TPU v7x, 32 devices: a whole 2x2x4 slice. The times are simulated.
32 devices in a mesh: row: 4 (over x, core), col: 8 (over z, y).
Axes of the slice: x: 2, y: 2, z: 4, core: 2. Of those that a mesh axis runs over, the one named last changes fastest.
Arguments:
- coupling: bfloat16 [32, 4096, 1024], P(('row', 'col')), may hold values from -0.09375 to 0.09375
- modes: bfloat16 [32, 200, 4096], P(('row', 'col')), may hold values from -6 to 6
- flexibility: float32 [32, 200], P(('row', 'col')), may hold values from 0.002 to 0.02
- widths: int32 [32], P(('row', 'col')), may hold values from 512 to 1024
- segments: int32 [32, 8], replicated, may hold values from 0 to 95, as said below
Outputs:
- interface: float32 [12288, 12288], P('row', 'col')
Inputs may be any that keep to these rules, and one draw needn't show every extreme that they name: `segments`: the 8 segment numbers of a substructure are distinct, and modulo 16 they are 8 cyclically consecutive residues. `widths`: columns at and beyond a substructure's width are padding.
All inputs are finite; a program needn't handle non-finite values.
Results may differ from a plain program's by a relative error of at most 0.0003.
Values sent between devices are 32-bit elements; how exact they have to be, the bound alone decides.
No kernel may reach another device: no remote copies, remote signals or barrier semaphores. Data moves between devices by JAX's collectives and lax.ppermute only.
A program may use at most 192 MiB of HBM per device.

v0:
```python
import jax
import jax.numpy as jnp
from jax import lax
from jax.sharding import PartitionSpec as P

TILE = 128
NG = 12288


def substructure_block(factor, modal_rows, weights, width):
    padded = factor.shape[1]
    columns = lax.broadcasted_iota(jnp.int32, (1, padded), 1)
    masked = jnp.where(columns < width, factor, jnp.zeros((), factor.dtype))
    static = lax.dot_general(
        masked, masked, (((0,), (0,)), ((), ())), preferred_element_type=jnp.float32
    )
    projected = jnp.dot(modal_rows, masked, preferred_element_type=jnp.float32)
    modal = lax.dot_general(
        projected * weights[:, None],
        projected,
        (((0,), (0,)), ((), ())),
        precision=lax.Precision.HIGHEST,
        preferred_element_type=jnp.float32,
    )
    return static - modal


def rank_among(residue_class):
    count = residue_class.shape[-1]
    places = lax.broadcasted_iota(jnp.int32, (count, count), 0)
    others = lax.broadcasted_iota(jnp.int32, (count, count), 1)
    same = residue_class[..., :, None] == residue_class[..., None, :]
    return jnp.sum(jnp.where(same & (others < places), 1, 0), axis=-1).astype(jnp.int32)


def body(coupling, modes, flexibility, widths, segments):
    row_count = lax.axis_size("row")
    col_count = lax.axis_size("col")
    device_total = row_count * col_count
    local_subs = coupling.shape[0]
    seg_count = coupling.shape[2] // TILE
    seg_total = NG // TILE
    row_tiles = seg_total // row_count
    col_tiles = seg_total // col_count
    row_cap = -(-seg_count // row_count)
    col_cap = -(-seg_count // col_count)
    member_cap = row_cap * col_cap
    capacity = local_subs * member_cap
    slots_all = device_total * capacity
    my_row = lax.axis_index("row")
    my_col = lax.axis_index("col")
    device_id = my_row * col_count + my_col
    blocks = jnp.stack(
        [
            substructure_block(coupling[0], modes[0], flexibility[0], widths[0]).reshape(
                seg_count, TILE, seg_count, TILE
            )
        ]
    )
    mine = lax.dynamic_slice_in_dim(segments, device_id * local_subs, local_subs, 0)
    own_diag = jnp.stack(
        [
            jnp.diagonal(blocks[:, index, :, index, :], axis1=1, axis2=2)
            for index in range(seg_count)
        ],
        axis=1,
    )
    seg_range = lax.broadcasted_iota(jnp.int32, (1, seg_total), 1)
    seg_hot = jnp.where(mine.reshape(-1)[:, None] == seg_range, 1.0, 0.0).astype(jnp.float32)
    partial_diag = lax.dot_general(
        seg_hot,
        own_diag.reshape(local_subs * seg_count, TILE),
        (((0,), (0,)), ((), ())),
        precision=lax.Precision.HIGHEST,
        preferred_element_type=jnp.float32,
    )
    summed_diag = lax.psum(partial_diag, ("row", "col"))
    row_diag = lax.dynamic_index_in_dim(
        summed_diag.reshape(row_tiles, row_count, TILE), my_row, 1, keepdims=False
    )
    col_diag = lax.dynamic_index_in_dim(
        summed_diag.reshape(col_tiles, col_count, TILE), my_col, 1, keepdims=False
    )
    row_res = mine % row_count
    col_res = mine % col_count
    row_rank = rank_among(row_res)
    col_rank = rank_among(col_res)
    member_ids = lax.broadcasted_iota(jnp.int32, (local_subs, seg_count, seg_count), 0)
    target = (
        (row_res[:, :, None] * col_count + col_res[:, None, :]) * capacity
        + member_ids * member_cap
        + row_rank[:, :, None] * col_cap
        + col_rank[:, None, :]
    )
    flat_target = target.reshape(-1)
    slot_ids = lax.broadcasted_iota(jnp.int32, (slots_all, flat_target.shape[0]), 0)
    matches = flat_target[None, :] == slot_ids
    tile_ids = lax.broadcasted_iota(jnp.int32, matches.shape, 1)
    source = jnp.sum(jnp.where(matches, tile_ids, 0), axis=1)
    filled = jnp.any(matches, axis=1)
    per_member = seg_count * seg_count
    member_src = source // per_member
    row_src = source % per_member // seg_count
    col_src = source % seg_count
    outgoing = blocks[member_src, row_src, :, col_src, :]
    outgoing = jnp.where(filled[:, None, None], outgoing, jnp.zeros((), jnp.float32))
    arriving = lax.all_to_all(outgoing, ("row", "col"), split_axis=0, concat_axis=0, tiled=True)
    every_row = segments % row_count
    every_col = segments % col_count
    every_row_rank = rank_among(every_row)
    every_col_rank = rank_among(every_col)
    subs_total = segments.shape[0]
    sub_ids = lax.broadcasted_iota(jnp.int32, (subs_total, seg_count, seg_count), 0)
    keeping = (every_row[:, :, None] == my_row) & (every_col[:, None, :] == my_col)
    placing = (
        sub_ids // local_subs * capacity
        + sub_ids % local_subs * member_cap
        + every_row_rank[:, :, None] * col_cap
        + every_col_rank[:, None, :]
    )
    local_tile = segments[:, :, None] // row_count * col_tiles + segments[:, None, :] // col_count
    keep_flat = keeping.reshape(-1)
    place_flat = placing.reshape(-1)
    tile_flat = local_tile.reshape(-1)
    tile_range = lax.broadcasted_iota(jnp.int32, (1, row_tiles * col_tiles), 1)
    slot_range = lax.broadcasted_iota(jnp.int32, (1, slots_all), 1)
    tile_hot = jnp.where(keep_flat[:, None] & (tile_flat[:, None] == tile_range), 1.0, 0.0).astype(
        jnp.float32
    )
    slot_hot = jnp.where(place_flat[:, None] == slot_range, 1.0, 0.0).astype(jnp.float32)
    routing = lax.dot_general(
        tile_hot,
        slot_hot,
        (((0,), (0,)), ((), ())),
        precision=lax.Precision.HIGHEST,
        preferred_element_type=jnp.float32,
    )
    routing = routing.reshape(row_tiles, col_tiles, slots_all)
    assembled = jnp.einsum(
        "rcp,pxy->rxcy",
        routing,
        arriving,
        precision=lax.Precision.HIGHEST,
        preferred_element_type=jnp.float32,
    )
    row_scale = 1.0 / jnp.sqrt(1.0 + jnp.abs(row_diag))
    col_scale = 1.0 / jnp.sqrt(1.0 + jnp.abs(col_diag))
    scaled = assembled * row_scale[:, :, None, None] * col_scale[None, None, :, :]
    return scaled.reshape(row_tiles * TILE, col_tiles * TILE)


def solution(mesh):
    in_specs = (
        P(("row", "col"), None, None),
        P(("row", "col"), None, None),
        P(("row", "col"), None),
        P(("row", "col")),
        P(),
    )
    out_specs = P("row", "col")
    return jax.shard_map(body, mesh=mesh, in_specs=in_specs, out_specs=out_specs, check_vma=False)
```

profile of v0, /device:TPU:0, one launch (start us, length us, event | category | flops | bytes accessed | tf_op | source)
XLA Modules:
  0.0 214.3 jit_solution(3561730800944807558)
XLA Ops:
  0.0 0.0 copy-start
  0.0 1.0 fusion.32
  1.0 0.2 select_reduce_fusion.3
  1.3 0.1 add.280
  1.3 0.1 add.273
  1.4 0.1 add.268
  1.5 0.1 add.269
  1.6 0.1 add.275
  1.6 0.1 add.276
  1.8 0.1 select_reduce_fusion.2
  1.9 0.1 fusion.28
  2.7 0.0 copy-done
  2.7 0.0 copy-start.3
  2.7 5.2 %fusion.1 = f32[1024,200]{0,1:T(8,128)S(1)} fusion(bf16[1,4096,1024]{2,1,0:T(8,128)(2,1)} %param.5, pred[1024]{0:T(1024)(128)(4,1)S(1)} %iota_compare_fusion.6, bf16[1,200,4096]{2,1,0:T(8,128)(2,1)S(1)} %copy-done), kind=kOutput, calls=%fused_computation.12 | convolution fusion | flops 1681915904 | bytes 10847232 | tf_op jit(solution)/shard_map/dot_general | solution.py:17
  8.0 0.0 copy-done.3
  8.0 3.8 %fusion.19 = f32[1024,1024]{1,0:T(8,128)S(1)} fusion(f32[1024,200]{0,1:T(8,128)S(1)} %fusion.1, f32[200]{0:T(256)S(1)} %bitcast.104), kind=kOutput, calls=%fused_computation.31 | convolution fusion | flops 2516787200 | bytes 5014304 | tf_op jit(solution)/shard_map/dot_general | solution.py:18
  11.8 16.1 %subtract_bitcast_fusion = f32[128,8,8,128]{3,1,2,0:T(8,128)S(1)} fusion(f32[1024,1024]{1,0:T(8,128)S(1)} %fusion.19, bf16[1,4096,1024]{2,1,0:T(8,128)(2,1)} %param.5, pred[1024]{0:T(1024)(128)(4,1)S(1)} %iota_compare_fusion.6), kind=kOutput, calls=%fused_computation.18 | convolution fusion | flops 8595177472 | bytes 16778240 | tf_op jit(solution)/shard_map/dot_general | solution.py:14
  27.9 1.0 copy.95
  28.9 2.8 %copy.65 = f32[1,8,128,8,128]{4,2,3,1,0:T(8,128)} copy(f32[1,8,128,8,128]{4,3,2,1,0:T(8,128)S(1)} %bitcast.93) | data formatting | bytes 8388608 | tf_op jit(solution)/shard_map/stack;reshape | solution.py:53
  31.7 5.0 %gather_fusion = f32[64,128,128]{2,1,0:T(8,128)} fusion(f32[1,8,128,8,128]{4,2,3,1,0:T(8,128)} %copy.65, s32[64]{0:T(128)S(1)} %fusion.53), kind=kCustom, calls=%fused_computation | custom fusion | bytes 8389376 | tf_op jit(solution)/shard_map/gather | solution.py:105
  36.7 4.5 %broadcast_select_fusion.3 = f32[64,128,128]{2,1,0:T(8,128)} fusion(f32[64,128,128]{2,1,0:T(8,128)} %gather_fusion, pred[64]{0:T(512)(128)(4,1)S(1)} %fusion.28), kind=kLoop, calls=%fused_computation.25 | loop fusion | flops 1048576 | bytes 8388672 | tf_op jit(solution)/shard_map/jit(_where)/select_n | solution.py:106
  41.2 0.0 copy-start.2
  41.2 7.7 %all-to-all-start = ((f32[64,128,128]{2,1,0:T(8,128)}), f32[64,128,128]{2,1,0:T(8,128)}, u32[]{:S(2)}, u32[]{:S(2)}) async-start(f32[64,128,128]{2,1,0:T(8,128)} %broadcast_select_fusion.3), calls=%async_computation | async-start | bytes 8388608 | tf_op jit(solution)/shard_map/all_to_all | solution.py:107
  48.9 0.0 copy-done.2
  48.9 0.1 copy.66
  49.0 0.1 copy.67
  49.1 0.1 select_reduce_fusion.1
  49.2 0.1 copy.70
  49.3 0.1 copy.68
  49.3 0.1 copy.71
  49.4 0.1 copy.69
  49.5 0.1 broadcast_and_fusion
  49.6 0.1 and.192
  49.7 0.1 broadcast_add_fusion
  49.8 0.1 add.292
  49.9 0.1 add_add_fusion
  50.0 0.1 add.298
  50.2 3.9 %fusion.8 = f32[288,64]{1,0:T(8,128)S(1)} fusion(s32[2048]{0:T(1024)S(1)} %add.292, pred[2048]{0:T(1024)(128)(4,1)S(1)} %and.192, s32[2048]{0:T(1024)S(1)} %add.298), kind=kOutput, calls=%fused_computation.21 | convolution fusion | flops 455016448 | bytes 92160 | tf_op jit(solution)/shard_map/dot_general | solution.py:131
  54.1 1.1 slice_bitcast_fusion
  55.2 1.2 gather_fusion.8
  56.5 1.2 gather_fusion.7
  57.7 1.2 gather_fusion.6
  59.0 1.2 gather_fusion.5
  60.2 1.2 gather_fusion.4
  61.5 1.2 gather_fusion.3
  62.7 1.2 gather_fusion.2
  64.0 1.2 gather_fusion.1
  65.3 0.3 fusion.35
  65.6 97.6 %psum.7 = f32[96,128]{1,0:T(8,128)S(1)} all-reduce(f32[96,128]{1,0:T(8,128)S(1)} %fusion.35), channel_id=1, replica_groups=mesh['row'=4,'col'=8] {'row','col'}, use_global_device_ids=true, to_apply=%region_6.7 | all-reduce | flops 12288 | bytes 98304 | tf_op jit(solution)/shard_map/psum | solution.py:77
  163.2 0.1 copy.93
  163.4 0.0 all-to-all-done
  163.4 19.8 %fusion = f32[24,128,12,128]{3,0,2,1:T(8,128)S(1)} fusion(f32[12,128]{1,0:T(8,128)S(1)} %fusion.31, f32[24,128]{0,1:T(8,128)S(1)} %rsqrt_bitcast_fusion, f32[64,128,128,1]{2,1,0,3:T(8,128)} %bitcast.6, f32[24,12,64]{2,1,0:T(8,128)S(1)} %reshape.565), kind=kOutput, calls=%fused_computation.11 | convolution fusion | flops 3633315840 | bytes 23160832 | tf_op jit(solution)/shard_map/rcp,pxy->rxcy/dot_general | solution.py:139
  183.2 10.4 %copy.91 = f32[24,128,12,128]{3,2,1,0:T(8,128)} copy(f32[24,128,12,128]{3,0,2,1:T(8,128)S(1)} %fusion) | data formatting | bytes 37748736 | tf_op jit(solution)/shard_map/reshape | solution.py:149
  193.6 0.0 copy-start.1
  193.7 20.7 %copy.111 = f32[384,8,12,128]{3,1,2,0:T(8,128)} copy(f32[384,8,12,128]{3,2,1,0:T(8,128)} %bitcast.92) | data formatting | bytes 37748736
  214.3 0.0 copy-done.1
  (16 shorter events, 0.2 us)
Async XLA Ops:
  0.0 2.7 %copy-start = (bf16[1,200,4096]{2,1,0:T(8,128)(2,1)S(1)}, bf16[1,200,4096]{2,1,0:T(8,128)(2,1)}, u32[]{:S(2)}) copy-start(bf16[1,200,4096]{2,1,0:T(8,128)(2,1)} %param.6) | copy-start | bytes 4915204
  2.7 5.3 %copy-start.3 = (f32[1,200]{1,0:T(1,128)S(1)}, f32[1,200]{1,0:T(1,128)}, u32[]{:S(2)}) copy-start(f32[1,200]{1,0:T(1,128)} %param.7) | copy-start | bytes 2404
  41.2 7.7 %copy-start.2 = (s32[32,8]{0,1:T(8,128)S(1)}, s32[32,8]{0,1:T(8,128)}, u32[]{:S(2)}) copy-start(s32[32,8]{0,1:T(8,128)} %param.9) | copy-start | bytes 3076
  41.2 122.2 %all-to-all-start = ((f32[64,128,128]{2,1,0:T(8,128)}), f32[64,128,128]{2,1,0:T(8,128)}, u32[]{:S(2)}, u32[]{:S(2)}) async-start(f32[64,128,128]{2,1,0:T(8,128)} %broadcast_select_fusion.3), calls=%async_computation | async-start | bytes 8388608 | tf_op jit(solution)/shard_map/all_to_all | solution.py:107
  193.6 20.7 %copy-start.1 = (bf16[1,200,4096]{2,1,0:T(8,128)(2,1)S(1)}, bf16[1,200,4096]{2,1,0:T(8,128)(2,1)}, u32[]{:S(2)}) copy-start(bf16[1,200,4096]{2,1,0:T(8,128)(2,1)} %param.6) | copy-start | bytes 4915204
where the time goes:
time: 215 us; the launch traced here: 214 us
  blocking collectives  97.6 us (45%)
  local copies, waits for them, and re-layouts  52.4 us (24%)
  matrix products  49.2 us (23%)
  starting transfers between devices  7.68 us (4%)
  other arithmetic  6.47 us (3%)
    psum x1, blocking collectives, body(): summed_diag = lax.psum(partial_diag, ('row', 'col'))  97.6 us
    unnamed x11, local copies, waits for them, and re-layouts  21.8 us
    dot_general x1, matrix products, body(): jnp.einsum('rcp,pxy->rxcy', routing, arriving, precision=lax.Precision.HI...  19.8 us
    dot_general x1, matrix products, substructure_block(): lax.dot_general(masked, masked, (((0,), (0,)), ((), ())), preferred_eleme...  16.1 us
    reshape x1, local copies, waits for them, and re-layouts, body(): return scaled.reshape(row_tiles * TILE, col_tiles * TILE)  10.4 us
    gather x8, local copies, waits for them, and re-layouts, body(): jnp.diagonal(blocks[:, index, :, index, :], axis1=1, axis2=2)  9.96 us
    all_to_all x1, starting transfers between devices, body(): lax.all_to_all(outgoing, ('row', 'col'), split_axis=0, concat_axis=0, til...  7.68 us
    dot_general x1, matrix products, substructure_block(): projected = jnp.dot(modal_rows, masked, preferred_element_type=jnp.float32)  5.24 us
  transfers between devices with their start and end apart: 1, of which 0 were waited for; matrix products, arithmetic and copies ran while one was open for 8% of the time, Pallas kernels for 0%

commit v1 on v0

--- a/solution.py
+++ b/solution.py
@@ -1,6 +1,11 @@
+import functools
+
 import jax
 import jax.numpy as jnp
 from jax import lax
+from jax.experimental import pallas as pl
+from jax.experimental.pallas import tpu as pltpu
+from jax.sharding import Mesh
 from jax.sharding import PartitionSpec as P
 
 TILE = 128
@@ -33,7 +38,7 @@
     return jnp.sum(jnp.where(same & (others < places), 1, 0), axis=-1).astype(jnp.int32)
 
 
-def body(coupling, modes, flexibility, widths, segments):
+def plain_body(coupling, modes, flexibility, widths, segments):
     row_count = lax.axis_size("row")
     col_count = lax.axis_size("col")
     device_total = row_count * col_count
@@ -149,13 +154,468 @@
     return scaled.reshape(row_tiles * TILE, col_tiles * TILE)
 
 
+AXES = ("row", "half", "low")
+CONTRACT_ROWS = (((0,), (0,)), ((), ()))
+VMEM_BYTES = 60 * 1024 * 1024
+
+
+def place():
+    row, half, low = (lax.axis_index(name) for name in AXES)
+    low_count = lax.axis_size("low")
+    device = (row * lax.axis_size("half") + half) * low_count + low
+    return row, half, low, device
+
+
+def order_segments(segs, order, half, device, seg_count):
+    per_half = seg_count // 2
+    for index in range(seg_count):
+        residue = lax.rem(segs[device, index], seg_count)
+        spot = lax.rem(residue, per_half) + jnp.where(residue // per_half == half, per_half, 0)
+        order[spot] = index
+
+
+def fetch(coupling, modes, held, held_modes, sems, order, segments):
+    copies = [pltpu.make_async_copy(modes, held_modes, sems.at[segments])]
+    copies[0].start()
+    for spot in range(segments):
+        source = coupling.at[:, pl.ds(pl.multiple_of(order[spot] * TILE, TILE), TILE)]
+        copy = pltpu.make_async_copy(source, held.at[:, pl.ds(spot * TILE, TILE)], sems.at[spot])
+        copy.start()
+        copies.append(copy)
+    return copies
+
+
+def mask_block(held, spot, index, width):
+    lanes = lax.broadcasted_iota(jnp.int32, (1, TILE), 1) + index * TILE
+    keep = jnp.where(lanes < width, 1.0, 0.0).astype(held.dtype)
+    part = pl.ds(spot * TILE, TILE)
+
+    @pl.when((index + 1) * TILE > width)
+    def _():
+        held[:, part] = held[:, part] * keep
+
+
+def project(held, held_modes, weights, total, left, right, columns):
+    count = held_modes.shape[0]
+    padded = left.shape[1]
+    spread = jnp.broadcast_to(weights[...], (TILE, padded)).T
+    for start in range(0, columns, 2 * TILE):
+        part = pl.ds(start, 2 * TILE)
+        total[...] = jnp.zeros_like(total)
+        total[pl.ds(0, count), :] = jnp.dot(
+            held_modes[...], held[:, part], preferred_element_type=jnp.float32
+        )
+        value = total[...]
+        scaled = -value * jnp.concatenate([spread, spread], axis=1)
+        high = value.astype(jnp.bfloat16)
+        scaled_high = scaled.astype(jnp.bfloat16)
+        right[0, :, part] = high
+        right[1, :, part] = (value - high.astype(jnp.float32)).astype(jnp.bfloat16)
+        left[0, :, part] = scaled_high
+        left[1, :, part] = (scaled - scaled_high.astype(jnp.float32)).astype(jnp.bfloat16)
+
+
+def product(held, left, right, rows, columns):
+    rows, columns = pl.ds(*rows), pl.ds(*columns)
+    dot = functools.partial(
+        lax.dot_general, dimension_numbers=CONTRACT_ROWS, preferred_element_type=jnp.float32
+    )
+    modal = (
+        dot(left[0, :, rows], right[1, :, columns])
+        + dot(left[1, :, rows], right[0, :, columns])
+        + dot(left[0, :, rows], right[0, :, columns])
+    )
+    return dot(held[:, rows], held[:, columns]) + modal
+
+
+def places_in_tile():
+    return (
+        lax.broadcasted_iota(jnp.int32, (TILE, TILE), 0),
+        lax.broadcasted_iota(jnp.int32, (TILE, TILE), 1),
+    )
+
+
+def tile_of(value, row, column):
+    return value[row * TILE : (row + 1) * TILE, column * TILE : (column + 1) * TILE]
+
+
+def upper_tiles(half_tiles):
+    return [(a, b) for a in range(half_tiles) for b in range(a + 1, half_tiles)]
+
+
+def symmetric_tiles(held, left, right, start, half_tiles):
+    tiles = {}
+    for a in range(0, half_tiles, 2):
+        for b in range(a, half_tiles, 2):
+            value = product(
+                held,
+                left,
+                right,
+                (start + a * TILE, 2 * TILE),
+                (start + b * TILE, 2 * TILE),
+            )
+            for i in range(2):
+                for j in range(2):
+                    if a + i <= b + j:
+                        tiles[a + i, b + j] = tile_of(value, i, j)
+    return tiles
+
+
+def far_kernel(segs, width, weights, coupling, modes, out, order, held, held_modes, total, left, right, sems):
+    _, half, _, device = place()
+    seg_count = segs.shape[1]
+    half_tiles = seg_count // 2
+    order_segments(segs, order, half, device, seg_count)
+    copies = fetch(coupling, modes, held, held_modes, sems, order, half_tiles)
+    for spot, copy in enumerate(copies):
+        copy.wait()
+        if spot:
+            mask_block(held, spot - 1, order[spot - 1], width[0])
+    project(held, held_modes, weights, total, left, right, half_tiles * TILE)
+    tiles = symmetric_tiles(held, left, right, 0, half_tiles)
+    rows, columns = places_in_tile()
+    uppers = upper_tiles(half_tiles)
+    for spot, pair in enumerate(uppers):
+        out[spot] = tiles[pair]
+    for a in range(0, half_tiles, 2):
+        out[len(uppers) + a // 2] = jnp.where(
+            rows <= columns, tiles[a, a], tiles[a + 1, a + 1].T
+        )
+
+
+def near_kernel(segs, width, weights, coupling, modes, mixed, own, diagonals, order, held, held_modes, total, left, right, sems):
+    _, half, _, device = place()
+    seg_count = segs.shape[1]
+    half_tiles = seg_count // 2
+    order_segments(segs, order, half, device, seg_count)
+    copies = fetch(coupling, modes, held, held_modes, sems, order, seg_count)
+    for spot, copy in enumerate(copies):
+        copy.wait()
+        if spot:
+            mask_block(held, spot - 1, order[spot - 1], width[0])
+    project(held, held_modes, weights, total, left, right, seg_count * TILE)
+    rows, columns = places_in_tile()
+    base = half_tiles * TILE
+    for a in range(0, half_tiles, 2):
+        for b in range(0, half_tiles, 2):
+            value = product(held, left, right, (base + a * TILE, 2 * TILE), (b * TILE, 2 * TILE))
+            for i in range(2):
+                for j in range(2):
+                    tile = tile_of(value, i, j)
+                    mixed[a + i, 1 - half, b + j] = tile
+                    mixed[b + j, half, a + i] = tile.T
+    near = symmetric_tiles(held, left, right, base, half_tiles)
+    for (a, b), tile in near.items():
+        own[a, b] = tile
+        if a != b:
+            own[b, a] = tile.T
+        else:
+            diagonals[pl.ds(half * half_tiles + a, 1), :] = jnp.sum(
+                jnp.where(rows == columns, tile, 0.0), axis=0, keepdims=True
+            )
+    for a in range(0, half_tiles, 2):
+        value = product(held, left, right, (a * TILE, 2 * TILE), (a * TILE, 2 * TILE))
+        for i in range(2):
+            diagonals[pl.ds((1 - half) * half_tiles + a + i, 1), :] = jnp.sum(
+                jnp.where(rows == columns, tile_of(value, i, i), 0.0), axis=0, keepdims=True
+            )
+
+
+def pack_kernel(own, diagonals, far, far_diagonals, *refs):
+    outs, tiles = refs[:-1], refs[-1]
+    row, half, low, _ = place()
+    half_tiles = own.shape[0]
+    rows, columns = places_in_tile()
+    uppers = upper_tiles(half_tiles)
+    for spot, (a, b) in enumerate(uppers):
+        tile = far[spot]
+        tiles[a, b] = tile
+        tiles[b, a] = tile.T
+    for a in range(0, half_tiles, 2):
+        tile = far[len(uppers) + a // 2]
+        turned = tile.T
+        tiles[a, a] = jnp.where(rows <= columns, tile, turned)
+        line = far_diagonals[pl.ds(half * half_tiles + a + 1, 1), :]
+        second = jnp.where(rows > columns, tile, turned)
+        tiles[a + 1, a + 1] = jnp.where(rows == columns, jnp.broadcast_to(line, (TILE, TILE)), second)
+    blank = jnp.zeros((1, TILE), jnp.float32)
+    for spot, out in enumerate(outs):
+        to_row, to_low = row ^ (spot // half_tiles), low ^ (spot % half_tiles)
+        out[pl.ds(0, TILE), :] = own[to_row, to_low]
+        out[pl.ds(TILE, TILE), :] = tiles[to_row, to_low]
+        lines = []
+        for source in (diagonals, far_diagonals):
+            lines += [
+                source[pl.ds(to_row, 1), :],
+                source[pl.ds(to_row + half_tiles, 1), :],
+                source[pl.ds(half * half_tiles + to_low, 1), :],
+                blank,
+            ]
+        out[pl.ds(2 * TILE, 8), :] = jnp.concatenate(lines, axis=0)
+
+
+def write_tiles(table, rows_at, tile_at, stage, out, row_scale, col_scale, sem):
+    count = stage.shape[0]
+
+    def piece(index):
+        row, column = table[rows_at, index], table[rows_at + 1, index]
+        return out.at[
+            pl.ds(pl.multiple_of(row * TILE, TILE), TILE),
+            pl.ds(pl.multiple_of(column * TILE, TILE), TILE),
+        ]
+
+    def emit(index, _):
+        @pl.when(table[rows_at + 3, index] == 1)
+        def _():
+            def more(state):
+                return state[0] < count
+
+            def add(state):
+                spot, value = state
+                return table[rows_at + 2, spot], value + tile_at(spot)
+
+            _, value = lax.while_loop(more, add, (table[rows_at + 2, index], tile_at(index)))
+            row, column = table[rows_at, index], table[rows_at + 1, index]
+            stage[index] = value * row_scale[row] * col_scale[pl.ds(column, 1), :]
+            pltpu.make_async_copy(stage.at[index], piece(index), sem).start()
+
+        return 0
+
+    lax.fori_loop(0, count, emit, 0)
+
+    def settle(index, _):
+        @pl.when(table[rows_at + 3, index] == 1)
+        def _():
+            pltpu.make_async_copy(stage.at[index], piece(index), sem).wait()
+
+        return 0
+
+    lax.fori_loop(0, count, settle, 0)
+
+
+def first_kernel(table, blank, *refs):
+    payload_count = len(refs) - 9
+    payloads = refs[:payload_count]
+    out, row_scale, col_scale, arrived, lines, stage, flat, sems, sem = refs[payload_count:]
+    del blank
+    copies = []
+    for spot, payload in enumerate(payloads):
+        copies.append(
+            pltpu.make_async_copy(payload.at[pl.ds(0, 2 * TILE), :], arrived.at[spot], sems.at[spot, 0])
+        )
+        copies.append(
+            pltpu.make_async_copy(payload.at[pl.ds(2 * TILE, 8), :], lines.at[spot], sems.at[spot, 1])
+        )
+    for copy in copies:
+        copy.start()
+    for copy in copies:
+        copy.wait()
+    row_count, col_count = row_scale.shape[0], col_scale.shape[0]
+    row_ids = lax.broadcasted_iota(jnp.int32, (row_count, TILE), 0)
+    col_ids = lax.broadcasted_iota(jnp.int32, (col_count, TILE), 0)
+    row_sum = jnp.zeros((row_count, TILE), jnp.float32)
+    col_sum = jnp.zeros((col_count, TILE), jnp.float32)
+    for spot in range(payload_count):
+        for side in range(2):
+            index = 2 * spot + side
+            for offset in range(2):
+                line = lines[spot, pl.ds(4 * side + offset, 1), :]
+                row_sum += jnp.where(row_ids == table[8 + offset, index], line, 0.0)
+            line = lines[spot, pl.ds(4 * side + 2, 1), :]
+            col_sum += jnp.where(col_ids == table[1, index], line, 0.0)
+    col_scale[...] = 1.0 / jnp.sqrt(1.0 + jnp.abs(col_sum))
+    flat[...] = 1.0 / jnp.sqrt(1.0 + jnp.abs(row_sum))
+    for index in range(row_count):
+        row_scale[index] = jnp.broadcast_to(flat[pl.ds(index, 1), :], (TILE, TILE)).T
+
+    def tile_at(index):
+        return arrived[index // 2, pl.ds(pl.multiple_of(lax.rem(index, 2) * TILE, TILE), TILE), :]
+
+    write_tiles(table, 0, tile_at, stage, out, row_scale, col_scale, sem)
+
+
+def second_kernel(table, mixed, row_scale, col_scale, filled, out, stage, sem):
+    del filled
+    write_tiles(table, 4, lambda index: mixed[index], stage, out, row_scale, col_scale, sem)
+
+
+def chain(rows, columns):
+    count = rows.shape[0]
+    same = (rows[:, None] == rows[None, :]) & (columns[:, None] == columns[None, :])
+    here = lax.broadcasted_iota(jnp.int32, (count, count), 0)
+    there = lax.broadcasted_iota(jnp.int32, (count, count), 1)
+    after = jnp.min(jnp.where(same & (there > here), there, count), axis=1)
+    first = jnp.where(jnp.any(same & (there < here), axis=1), 0, 1)
+    return [rows, columns, after, first]
+
+
+def placements(segments, row, half, low, row_count, low_count):
+    col_count = 2 * low_count
+    residue = segments % col_count
+
+    def with_residue(wanted):
+        return jnp.sum(jnp.where(residue == wanted, segments, 0), axis=1)
+
+    near_rows = with_residue(row + half * low_count) // row_count
+    far_rows = with_residue(row + (1 - half) * low_count) // row_count
+    columns = with_residue(half * low_count + low) // col_count
+    spots = jnp.arange(row_count * low_count)
+    source_row, source_low = row ^ (spots // low_count), low ^ (spots % low_count)
+    sources = jnp.stack(
+        [(source_row * 2 + side) * low_count + source_low for side in (half, 1 - half)], axis=1
+    ).reshape(-1)
+    lower = jnp.where(half == 0, near_rows, far_rows)
+    upper = jnp.where(half == 0, far_rows, near_rows)
+    return jnp.stack(
+        chain(near_rows[sources], columns[sources])
+        + chain(far_rows, columns)
+        + [lower[sources], upper[sources]]
+    ).astype(jnp.int32)
+
+
+def whole(memory=pltpu.VMEM):
+    return pl.BlockSpec(memory_space=memory)
+
+
+def fast_body(coupling, modes, flexibility, widths, segments):
+    return exchange(coupling, modes, flexibility, widths, segments)
+
+
+def exchange(coupling, modes, flexibility, widths, segments):
+    row_count, low_count = lax.axis_size("row"), lax.axis_size("low")
+    row, half, low, _ = place()
+    interior, padded = coupling.shape[1:]
+    mode_count = modes.shape[1]
+    mode_pad = -(-mode_count // 256) * 256
+    seg_count = padded // TILE
+    half_tiles = seg_count // 2
+    seg_total = NG // TILE
+    row_tiles, col_tiles = seg_total // row_count, seg_total // (2 * low_count)
+    weights = jnp.pad(flexibility, ((0, 0), (0, mode_pad - mode_count)))
+    f32, bf16 = jnp.float32, jnp.bfloat16
+    params = pltpu.CompilerParams(vmem_limit_bytes=VMEM_BYTES)
+    inputs = (segments, widths, weights, coupling[0], modes[0])
+    in_specs = [whole(pltpu.SMEM), whole(pltpu.SMEM), whole(), whole(pl.ANY), whole(pl.ANY)]
+
+    def scratch(count):
+        return [
+            pltpu.SMEM((seg_count,), jnp.int32),
+            pltpu.VMEM((interior, count * TILE), bf16),
+            pltpu.VMEM((mode_count, interior), bf16),
+            pltpu.VMEM((mode_pad, 2 * TILE), f32),
+            pltpu.VMEM((2, mode_pad, count * TILE), bf16),
+            pltpu.VMEM((2, mode_pad, count * TILE), bf16),
+            pltpu.SemaphoreType.DMA((count + 1,)),
+        ]
+
+    far_count = len(upper_tiles(half_tiles)) + half_tiles // 2
+    far_tiles = pl.pallas_call(
+        far_kernel,
+        out_shape=jax.ShapeDtypeStruct((far_count, TILE, TILE), f32),
+        in_specs=in_specs,
+        out_specs=whole(),
+        scratch_shapes=scratch(half_tiles),
+        compiler_params=params,
+        name="far",
+        cost_estimate=pl.CostEstimate(flops=4 * 10**9, bytes_accessed=6 * 10**6, transcendentals=0),
+    )(*inputs)
+    swap = [(0, 1), (1, 0)]
+    far_in = lax.ppermute(far_tiles, "half", swap)
+    mixed, own, diagonals = pl.pallas_call(
+        near_kernel,
+        out_shape=[
+            jax.ShapeDtypeStruct((row_count, 2, low_count, TILE, TILE), f32),
+            jax.ShapeDtypeStruct((half_tiles, half_tiles, TILE, TILE), f32),
+            jax.ShapeDtypeStruct((seg_count, TILE), f32),
+        ],
+        in_specs=in_specs,
+        out_specs=[whole()] * 3,
+        scratch_shapes=scratch(seg_count),
+        compiler_params=params,
+        name="near",
+        cost_estimate=pl.CostEstimate(flops=8 * 10**9, bytes_accessed=10**7, transcendentals=0),
+    )(*inputs)
+    far_diagonals = lax.ppermute(diagonals, "half", swap)
+    sources = row_count * 2 * low_count
+    mixed_in = lax.all_to_all(
+        mixed.reshape(sources, TILE, TILE), AXES, split_axis=0, concat_axis=0, tiled=True
+    )
+    payload = jax.ShapeDtypeStruct((2 * TILE + 8, TILE), f32)
+    in_half = row_count * low_count
+    payloads = pl.pallas_call(
+        pack_kernel,
+        out_shape=[payload] * in_half,
+        in_specs=[whole()] * 4,
+        out_specs=[whole()] * in_half,
+        scratch_shapes=[pltpu.VMEM((half_tiles, half_tiles, TILE, TILE), f32)],
+        compiler_params=params,
+        name="pack",
+        cost_estimate=pl.CostEstimate(flops=10**6, bytes_accessed=6 * 10**6, transcendentals=0),
+    )(own, diagonals, far_in, far_diagonals)
+    arrived = [payloads[0]]
+    for spot in range(1, in_half):
+        arrived.append(
+            lax.ppermute(payloads[spot], ("row", "low"), [(i, i ^ spot) for i in range(in_half)])
+        )
+    table = placements(segments, row, half, low, row_count, low_count)
+    blank = jnp.zeros((row_tiles * TILE, col_tiles * TILE), f32)
+    shape = jax.ShapeDtypeStruct(blank.shape, f32)
+    filled, row_scale, col_scale = pl.pallas_call(
+        first_kernel,
+        out_shape=[
+            shape,
+            jax.ShapeDtypeStruct((row_tiles, TILE, TILE), f32),
+            jax.ShapeDtypeStruct((col_tiles, TILE), f32),
+        ],
+        in_specs=[whole(pltpu.SMEM), whole(pl.ANY)] + [whole(pl.ANY)] * in_half,
+        out_specs=[whole(pl.ANY), whole(), whole()],
+        scratch_shapes=[
+            pltpu.VMEM((in_half, 2 * TILE, TILE), f32),
+            pltpu.VMEM((in_half, 8, TILE), f32),
+            pltpu.VMEM((2 * in_half, TILE, TILE), f32),
+            pltpu.VMEM((row_tiles, TILE), f32),
+            pltpu.SemaphoreType.DMA((in_half, 2)),
+            pltpu.SemaphoreType.DMA,
+        ],
+        input_output_aliases={1: 0},
+        compiler_params=params,
+        name="first",
+        cost_estimate=pl.CostEstimate(flops=10**6, bytes_accessed=6 * 10**6, transcendentals=0),
+    )(table, blank, *arrived)
+    return pl.pallas_call(
+        second_kernel,
+        out_shape=shape,
+        in_specs=[whole(pltpu.SMEM), whole(), whole(), whole(), whole(pl.ANY)],
+        out_specs=whole(pl.ANY),
+        scratch_shapes=[pltpu.VMEM((sources, TILE, TILE), f32), pltpu.SemaphoreType.DMA],
+        input_output_aliases={4: 0},
+        compiler_params=params,
+        name="second",
+        cost_estimate=pl.CostEstimate(flops=10**6, bytes_accessed=6 * 10**6, transcendentals=0),
+    )(table, mixed_in, row_scale, col_scale, filled)
+
+
 def solution(mesh):
-    in_specs = (
-        P(("row", "col"), None, None),
-        P(("row", "col"), None, None),
-        P(("row", "col"), None),
-        P(("row", "col")),
-        P(),
-    )
-    out_specs = P("row", "col")
-    return jax.shard_map(body, mesh=mesh, in_specs=in_specs, out_specs=out_specs, check_vma=False)
+    row_count, col_count = mesh.shape["row"], mesh.shape["col"]
+    low_count = col_count // 2
+    split = Mesh(mesh.devices.reshape(row_count, 2, low_count), AXES)
+
+    def run(coupling, modes, flexibility, widths, segments):
+        fits = (
+            segments.shape[1] == col_count
+            and row_count == low_count
+            and row_count & (row_count - 1) == 0
+            and segments.shape[0] == row_count * col_count
+        )
+        axes, used, body = (AXES, split, fast_body) if fits else (("row", "col"), mesh, plain_body)
+        in_specs = (P(axes, None, None), P(axes, None, None), P(axes, None), P(axes), P())
+        step = jax.shard_map(
+            body,
+            mesh=used,
+            in_specs=in_specs,
+            out_specs=P("row", axes[1:]),
+            check_vma=False,
+        )
+        return step(coupling, modes, flexibility, widths, segments)
+
+    return run

time: 215 us -> 157 us (0.73)
  blocking collectives: 97.6 us -> 0 us
  waiting for transfers between devices: 0.01 us -> 72.3 us
  matrix products: 49.2 us -> 0 us
  Pallas kernels: 0 us -> 35 us
  local copies, waits for them, and re-layouts: 52.4 us -> 18.2 us
  starting transfers between devices: 7.68 us -> 28.5 us
  other arithmetic: 6.47 us -> 0.84 us
    psum x1 -> x0, blocking collectives: 97.6 us -> none  [body(): summed_diag = lax.psum(partial_diag, ('row', 'col'))]
    ppermute x0 -> x17, waiting for transfers between devices: none -> 72.3 us  [the longest x1 60.1 us: exchange(): far_diagonals = lax.ppermute(diagonals, 'half', swap)]
    dot_general x6 -> x0, matrix products: 49.2 us -> none  [the longest x1 19.8 us: body(): jnp.einsum('rcp,pxy->rxcy', routing, arriving, precision=lax.Precision.HI...]
    pallas_call x0 -> x5, Pallas kernels: none -> 35 us  [the longest x1 14.6 us: exchange(): pl.pallas_call(near_kernel, out_shape=[jax.ShapeDtypeStruct((row_count, 2...]
    ppermute x0 -> x17, starting transfers between devices: none -> 20.9 us  [the longest x15 17.9 us: exchange(): lax.ppermute(payloads[spot], ('row', 'low'), [(i, i ^ spot) for i in rang...]
    unnamed x11 -> x31, local copies, waits for them, and re-layouts: 21.8 us -> 3.54 us
    gather x9 -> x4, local copies, waits for them, and re-layouts: 14.9 us -> 2.8 us  [the longest x1 0.7 us: placements(): lower[sources]]
    reshape x2 -> x1, local copies, waits for them, and re-layouts: 10.4 us -> 0.09 us  [placements(): sources = jnp.stack([(source_row * 2 + side) * low_count + source_low for...]
  transfers between devices with their start and end apart: 1 -> 18, of which waited for: 0 -> 6; matrix products, arithmetic and copies ran while one was open for 8% -> 9% of each run, Pallas kernels for 0% -> 11%
where the time goes in v1:
time: 157 us; the launch traced here: 156 us
  waiting for transfers between devices  72.3 us (46%)
  Pallas kernels  35 us (22%)
  starting transfers between devices  28.5 us (18%)
  local copies, waits for them, and re-layouts  18.2 us (12%)
    ppermute x1, waiting for transfers between devices, exchange(): far_diagonals = lax.ppermute(diagonals, 'half', swap)  60.1 us
    ppermute x15, starting transfers between devices, exchange(): lax.ppermute(payloads[spot], ('row', 'low'), [(i, i ^ spot) for i in rang...  17.9 us
    pallas_call x1, Pallas kernels, exchange(): pl.pallas_call(near_kernel, out_shape=[jax.ShapeDtypeStruct((row_count, 2...  14.6 us
    ppermute x15, waiting for transfers between devices, exchange(): lax.ppermute(payloads[spot], ('row', 'low'), [(i, i ^ spot) for i in rang...  12.2 us
    broadcast_in_dim x1, local copies, waits for them, and re-layouts, exchange(): blank = jnp.zeros((row_tiles * TILE, col_tiles * TILE), f32)  9.26 us
    pallas_call x1, Pallas kernels, exchange(): pl.pallas_call(far_kernel, out_shape=jax.ShapeDtypeStruct((far_count, TIL...  7.7 us
    all_to_all x1, starting transfers between devices, exchange(): lax.all_to_all(mixed.reshape(sources, TILE, TILE), AXES, split_axis=0, co...  7.6 us
    pallas_call x1, Pallas kernels, exchange(): pl.pallas_call(first_kernel, out_shape=[shape, jax.ShapeDtypeStruct((row_...  6.1 us
  transfers between devices with their start and end apart: 18, of which 6 were waited for; matrix products, arithmetic and copies ran while one was open for 9% of the time, Pallas kernels for 11%

profile of v1, /device:TPU:0, one launch (start us, length us, event | category | flops | bytes accessed | tf_op | source)
XLA Modules:
  0.0 156.0 jit_solution(13755198822830688818)
XLA Ops:
  0.7 1.4 copy.16.segs
  2.0 1.2 pad.4.weights
  3.2 14.6 %near.1 = (f32[4,2,4,128,128]{4,3,2,1,0:T(8,128)}, f32[4,4,128,128]{3,2,1,0:T(8,128)}, f32[8,128]{1,0:T(8,128)}) custom-call(s32[32,8]{1,0:T(8,128)} %copy.16.segs, s32[1]{0:T(128)S(6)} %copy.20.width, f32[1,256]{1,0:T(1,128)} %pad.4.weights, bf16[4096,1024]{1,0:T(8,128)(2,1)} %bitcast.38, bf16[200,4096]{1,0:T(8,128)(2,1)} %bitcast.40), custom_call_target="tpu_custom_call" | custom-call | flops 8000000000 | bytes 10000000 | tf_op jit(solution)/shard_map/near/pallas_call | solution.py:524
  17.8 7.6 %all-to-all-start = ((f32[32,128,128]{2,1,0:T(8,128)}), f32[32,128,128]{2,1,0:T(8,128)S(1)}, u32[]{:S(2)}, u32[]{:S(2)}) async-start(f32[32,128,128]{2,1,0:T(8,128)} %bitcast.31), calls=%async_computation | async-start | bytes 4194304 | tf_op jit(solution)/shard_map/all_to_all | solution.py:540
  25.4 0.0 copy-start.13
  25.4 0.0 copy-start.12
  25.4 7.7 %far.1 = f32[8,128,128]{2,1,0:T(8,128)} custom-call(s32[32,8]{1,0:T(8,128)} %copy.16.segs, s32[1]{0:T(128)S(6)} %copy.20.width, f32[1,256]{1,0:T(1,128)} %pad.4.weights, bf16[4096,1024]{1,0:T(8,128)(2,1)} %bitcast.39, bf16[200,4096]{1,0:T(8,128)(2,1)} %bitcast.41), custom_call_target="tpu_custom_call" | custom-call | flops 4000000000 | bytes 6000000 | tf_op jit(solution)/shard_map/far/pallas_call | solution.py:512
  33.1 2.7 %collective-permute-start = (f32[8,128,128]{2,1,0:T(8,128)}, f32[8,128,128]{2,1,0:T(8,128)S(1)}, u32[]{:S(2)}, u32[]{:S(2)}) collective-permute-start(f32[8,128,128]{2,1,0:T(8,128)} %far.1), channel_id=1, source_target_pairs={{0,4},{4,0},{1,5},{5,1},{2,6},{6,2},{3,7},{7,3},{8,12},{12,8},{9,1... | collective-permute-start | bytes 1572872 | tf_op jit(solution)/shard_map/ppermute | solution.py:523
  35.9 0.0 copy-done.13
  35.9 0.3 collective-permute-start.1
  36.1 0.0 copy-done.12
  36.2 0.2 fusion.5
  36.4 0.1 copy.15
  36.5 0.1 reshape.267
  36.6 60.1 %collective-permute-done.1.far_diagonals = f32[8,128]{1,0:T(8,128)S(1)} collective-permute-done((f32[8,128]{1,0:T(8,128)S(1)}, f32[8,128]{1,0:T(8,128)S(1)}, u32[]{:S(2)}, u32[]{:S(2)}) %collective-permute-start.1) | collective-permute-done | bytes 4128 | tf_op jit(solution)/shard_map/ppermute | solution.py:538
  96.7 0.0 collective-permute-done.far
  96.7 0.6 copy-done.14
  97.3 0.2 copy-done.1
  97.5 3.0 %pack.1 = (f32[264,128]{1,0:T(8,128)}, f32[264,128]{1,0:T(8,128)}, f32[264,128]{1,0:T(8,128)}, f32[264,128]{1,0:T(8,128)}, f32[264,128]{1,0:T(8,128)}, /*index=5...) custom-call(f32[4,4,128,128]{3,2,1,0:T(8,128)} %get-tuple-element.28, ...), custom_call_target="tpu_custom_call" | custom-call | flops 1000000 | bytes 6000000 | tf_op jit(solution)/shard_map/pack/pallas_call | solution.py:545
  100.5 1.5 collective-permute-start.2
  102.0 0.0 collective-permute-start.3
  102.0 2.0 %collective-permute-start.4 = (f32[264,128]{1,0:T(8,128)}, f32[264,128]{1,0:T(8,128)S(1)}, u32[]{:S(2)}, u32[]{:S(2)}) collective-permute-start(f32[264,128]{1,0:T(8,128)} %get-tuple-element.33), channel_id=1, source_target_pairs={{0,3},{1,2},{2,1},{3,0},{8,11},{9,10},{10,9},{11,8},{16,19},{17,18... | collective-permute-start | bytes 405512 | tf_op jit(solution)/shard_map/ppermute | solution.py:558
  104.0 0.0 collective-permute-start.5
  104.0 1.6 %collective-permute-start.6 = (f32[264,128]{1,0:T(8,128)}, f32[264,128]{1,0:T(8,128)S(1)}, u32[]{:S(2)}, u32[]{:S(2)}) collective-permute-start(f32[264,128]{1,0:T(8,128)} %get-tuple-element.35), channel_id=1, source_target_pairs={{0,9},{1,8},{2,11},{3,10},{8,1},{9,0},{10,3},{11,2},{16,25},{17,24... | collective-permute-start | bytes 405512 | tf_op jit(solution)/shard_map/ppermute | solution.py:558
  105.6 0.7 gather_fusion.1
  106.3 0.7 gather_fusion
  107.0 0.2 fusion.4
  107.2 0.0 collective-permute-done.2.refs_1_
  107.2 0.0 copy-start.2
  107.2 0.1 collective-permute-start.7
  107.3 1.1 collective-permute-done.3.refs_2_
  108.4 0.6 collective-permute-start.8
  109.0 0.8 collective-permute-done.4.refs_3_
  109.8 1.5 collective-permute-start.9
  111.3 0.0 collective-permute-done.5.refs_4_
  111.3 1.5 collective-permute-start.10
  112.8 0.0 collective-permute-done.6.refs_5_
  112.8 1.3 collective-permute-start.11
  114.1 0.0 collective-permute-done.7.refs_6_
  114.1 1.7 %collective-permute-start.12 = (f32[264,128]{1,0:T(8,128)}, f32[264,128]{1,0:T(8,128)}, u32[]{:S(2)}, u32[]{:S(2)}) collective-permute-start(f32[264,128]{1,0:T(8,128)} %get-tuple-element.41), channel_id=1, source_target_pairs={{0,19},{1,18},{2,17},{3,16},{8,27},{9,26},{10,25},{11,24},{16,3},{... | collective-permute-start | bytes 405512 | tf_op jit(solution)/shard_map/ppermute | solution.py:558
  115.8 1.7 %collective-permute-done.8.refs_7_ = f32[264,128]{1,0:T(8,128)S(1)} collective-permute-done((f32[264,128]{1,0:T(8,128)}, f32[264,128]{1,0:T(8,128)S(1)}, u32[]{:S(2)}, u32[]{:S(2)}) %collective-permute-start.8) | collective-permute-done | bytes 135200 | tf_op jit(solution)/shard_map/ppermute | solution.py:558
  117.4 1.1 collective-permute-start.13
  118.6 0.0 collective-permute-done.9.refs_8_
  118.6 1.7 %collective-permute-start.14 = (f32[264,128]{1,0:T(8,128)}, f32[264,128]{1,0:T(8,128)}, u32[]{:S(2)}, u32[]{:S(2)}) collective-permute-start(f32[264,128]{1,0:T(8,128)} %get-tuple-element.43), channel_id=1, source_target_pairs={{0,25},{1,24},{2,27},{3,26},{8,17},{9,16},{10,19},{11,18},{16,9},{... | collective-permute-start | bytes 405512 | tf_op jit(solution)/shard_map/ppermute | solution.py:558
  120.3 4.7 %collective-permute-done.10.refs_9_ = f32[264,128]{1,0:T(8,128)S(1)} collective-permute-done((f32[264,128]{1,0:T(8,128)}, f32[264,128]{1,0:T(8,128)S(1)}, u32[]{:S(2)}, u32[]{:S(2)}) %collective-permute-start.10) | collective-permute-done | bytes 135200 | tf_op jit(solution)/shard_map/ppermute | solution.py:558
  125.0 0.8 collective-permute-start.15
  125.8 0.0 collective-permute-done.11.refs_10_
  125.8 2.6 %collective-permute-start.16 = (f32[264,128]{1,0:T(8,128)}, f32[264,128]{1,0:T(8,128)}, u32[]{:S(2)}, u32[]{:S(2)}) collective-permute-start(f32[264,128]{1,0:T(8,128)} %get-tuple-element.45), channel_id=1, source_target_pairs={{0,27},{1,26},{2,25},{3,24},{8,19},{9,18},{10,17},{11,16},{16,11},... | collective-permute-start | bytes 405512 | tf_op jit(solution)/shard_map/ppermute | solution.py:558
  128.4 0.2 select_reduce_fusion
  128.6 0.7 gather_fusion.3
  129.3 0.7 gather_fusion.2
  130.0 0.2 select_reduce_fusion.1
  130.2 1.2 stack.37.table
  131.4 0.0 collective-permute-done.12.refs_11_
  131.4 0.0 collective-permute-done.13.refs_12_
  131.4 3.8 %collective-permute-done.14.refs_13_ = f32[264,128]{1,0:T(8,128)} collective-permute-done((f32[264,128]{1,0:T(8,128)}, f32[264,128]{1,0:T(8,128)}, u32[]{:S(2)}, u32[]{:S(2)}) %collective-permute-start.14) | collective-permute-done | bytes 135200 | tf_op jit(solution)/shard_map/ppermute | solution.py:558
  135.3 0.0 collective-permute-done.15.refs_14_
  135.3 0.0 collective-permute-done.16.refs_15_
  135.3 9.3 %broadcast_in_dim.18.blank = f32[3072,1536]{1,0:T(8,128)} broadcast(f32[]{:T(128)} %constant.97.clone.1), dimensions={} | broadcast | bytes 18874372 | tf_op jit(solution)/shard_map/broadcast_in_dim | solution.py:561
  144.6 0.0 copy-done.3
  144.6 6.1 %first.1 = (f32[3072,1536]{1,0:T(8,128)}, f32[24,128,128]{2,1,0:T(8,128)}, f32[12,128]{1,0:T(8,128)}) custom-call(s32[10,32]{1,0:T(8,128)} %stack.37.table, f32[3072,1536]{1,0:T(8,128)} %broadcast_in_dim.18.blank, f32[264,128]{1,0:T(8,128)} %get-tuple-element.30.refs_0_, f32[264,128]{1,0:T(8,128)} %copy-done.2, ...), custom_call_target="tpu_custom_call", output_to_operand_aliasing={{0}: (1, {})} | custom-call | flops 1000000 | bytes 6000000 | tf_op jit(solution)/shard_map/first/pallas_call | solution.py:563
  150.7 0.0 all-to-all-done.mixed
  150.7 1.3 copy-done
  152.1 3.7 %second.1 = f32[3072,1536]{1,0:T(8,128)} custom-call(s32[10,32]{1,0:T(8,128)} %stack.37.table, f32[32,128,128]{2,1,0:T(8,128)} %copy-done, f32[24,128,128]{2,1,0:T(8,128)} %get-tuple-element.46.row_scale, f32[12,128]{1,0:T(8,128)} %get-tuple-element.47.col_scale, f32[3072,1536]{1,0:T(8,128)} %get-tuple-element.48.filled), custom_call_target="tpu_custom_call", output_to_operand_aliasing={{}: (4, {})} | custom-call | flops 1000000 | bytes 6000000 | tf_op jit(solution)/shard_map/second/pallas_call | solution.py:585
  (31 shorter events, 0.1 us)
Async XLA Ops:
  17.8 132.9 %all-to-all-start = ((f32[32,128,128]{2,1,0:T(8,128)}), f32[32,128,128]{2,1,0:T(8,128)S(1)}, u32[]{:S(2)}, u32[]{:S(2)}) async-start(f32[32,128,128]{2,1,0:T(8,128)} %bitcast.31), calls=%async_computation | async-start | bytes 4194304 | tf_op jit(solution)/shard_map/all_to_all | solution.py:540
  25.4 10.5 %copy-start.13 = (f32[8,128]{1,0:T(8,128)S(1)}, f32[8,128]{1,0:T(8,128)}, u32[]{:S(2)}) copy-start(f32[8,128]{1,0:T(8,128)} %get-tuple-element.29.diagonals) | copy-start | bytes 12292
  25.4 10.7 %copy-start.12 = (s32[32,8]{0,1:T(8,128)S(1)}, s32[32,8]{0,1:T(8,128)}, u32[]{:S(2)}) copy-start(s32[32,8]{0,1:T(8,128)} %param.9) | copy-start | bytes 3076
  33.1 63.6 %collective-permute-start = (f32[8,128,128]{2,1,0:T(8,128)}, f32[8,128,128]{2,1,0:T(8,128)S(1)}, u32[]{:S(2)}, u32[]{:S(2)}) collective-permute-start(f32[8,128,128]{2,1,0:T(8,128)} %far.1), channel_id=1, source_target_pairs={{0,4},{4,0},{1,5},{5,1},{2,6},{6,2},{3,7},{7,3},{8,12},{12,8},{9,1... | collective-permute-start | bytes 1572872 | tf_op jit(solution)/shard_map/ppermute | solution.py:523
  35.9 60.9 %collective-permute-start.1 = (f32[8,128]{1,0:T(8,128)S(1)}, f32[8,128]{1,0:T(8,128)S(1)}, u32[]{:S(2)}, u32[]{:S(2)}) collective-permute-start(f32[8,128]{1,0:T(8,128)S(1)} %copy-done.13), channel_id=1, source_target_pairs={{0,4},{4,0},{1,5},{5,1},{2,6},{6,2},{3,7},{7,3},{8,12},{12,8},{9,1... | collective-permute-start | bytes 12296 | tf_op jit(solution)/shard_map/ppermute | solution.py:538
  96.7 0.6 copy-start.14
  96.7 0.8 copy-start.1
  100.5 6.7 %collective-permute-start.2 = (f32[264,128]{1,0:T(8,128)}, f32[264,128]{1,0:T(8,128)S(1)}, u32[]{:S(2)}, u32[]{:S(2)}) collective-permute-start(f32[264,128]{1,0:T(8,128)} %get-tuple-element.31), channel_id=1, source_target_pairs={{0,1},{1,0},{2,3},{3,2},{8,9},{9,8},{10,11},{11,10},{16,17},{17,16... | collective-permute-start | bytes 405512 | tf_op jit(solution)/shard_map/ppermute | solution.py:558
  102.0 6.4 %collective-permute-start.3 = (f32[264,128]{1,0:T(8,128)}, f32[264,128]{1,0:T(8,128)S(1)}, u32[]{:S(2)}, u32[]{:S(2)}) collective-permute-start(f32[264,128]{1,0:T(8,128)} %get-tuple-element.32), channel_id=1, source_target_pairs={{0,2},{1,3},{2,0},{3,1},{8,10},{9,11},{10,8},{11,9},{16,18},{17,19... | collective-permute-start | bytes 405512 | tf_op jit(solution)/shard_map/ppermute | solution.py:558
  102.0 7.8 %collective-permute-start.4 = (f32[264,128]{1,0:T(8,128)}, f32[264,128]{1,0:T(8,128)S(1)}, u32[]{:S(2)}, u32[]{:S(2)}) collective-permute-start(f32[264,128]{1,0:T(8,128)} %get-tuple-element.33), channel_id=1, source_target_pairs={{0,3},{1,2},{2,1},{3,0},{8,11},{9,10},{10,9},{11,8},{16,19},{17,18... | collective-permute-start | bytes 405512 | tf_op jit(solution)/shard_map/ppermute | solution.py:558
  104.0 7.3 %collective-permute-start.5 = (f32[264,128]{1,0:T(8,128)}, f32[264,128]{1,0:T(8,128)S(1)}, u32[]{:S(2)}, u32[]{:S(2)}) collective-permute-start(f32[264,128]{1,0:T(8,128)} %get-tuple-element.34), channel_id=1, source_target_pairs={{0,8},{1,9},{2,10},{3,11},{8,0},{9,1},{10,2},{11,3},{16,24},{17,25... | collective-permute-start | bytes 405512 | tf_op jit(solution)/shard_map/ppermute | solution.py:558
  104.0 8.8 %collective-permute-start.6 = (f32[264,128]{1,0:T(8,128)}, f32[264,128]{1,0:T(8,128)S(1)}, u32[]{:S(2)}, u32[]{:S(2)}) collective-permute-start(f32[264,128]{1,0:T(8,128)} %get-tuple-element.35), channel_id=1, source_target_pairs={{0,9},{1,8},{2,11},{3,10},{8,1},{9,0},{10,3},{11,2},{16,25},{17,24... | collective-permute-start | bytes 405512 | tf_op jit(solution)/shard_map/ppermute | solution.py:558
  107.2 37.4 %copy-start.2 = (f32[264,128]{1,0:T(8,128)}, f32[264,128]{1,0:T(8,128)S(1)}, u32[]{:S(2)}) copy-start(f32[264,128]{1,0:T(8,128)S(1)} %collective-permute-done.2.refs_1_) | copy-start | bytes 405508
  107.2 6.9 %collective-permute-start.7 = (f32[264,128]{1,0:T(8,128)}, f32[264,128]{1,0:T(8,128)S(1)}, u32[]{:S(2)}, u32[]{:S(2)}) collective-permute-start(f32[264,128]{1,0:T(8,128)} %get-tuple-element.36), channel_id=1, source_target_pairs={{0,10},{1,11},{2,8},{3,9},{8,2},{9,3},{10,0},{11,1},{16,26},{17,27... | collective-permute-start | bytes 405512 | tf_op jit(solution)/shard_map/ppermute | solution.py:558
  108.4 36.2 %copy-start.3 = (f32[264,128]{1,0:T(8,128)}, f32[264,128]{1,0:T(8,128)S(1)}, u32[]{:S(2)}) copy-start(f32[264,128]{1,0:T(8,128)S(1)} %collective-permute-done.3.refs_2_) | copy-start | bytes 405508
  108.4 9.0 %collective-permute-start.8 = (f32[264,128]{1,0:T(8,128)}, f32[264,128]{1,0:T(8,128)S(1)}, u32[]{:S(2)}, u32[]{:S(2)}) collective-permute-start(f32[264,128]{1,0:T(8,128)} %get-tuple-element.37), channel_id=1, source_target_pairs={{0,11},{1,10},{2,9},{3,8},{8,3},{9,2},{10,1},{11,0},{16,27},{17,26... | collective-permute-start | bytes 405512 | tf_op jit(solution)/shard_map/ppermute | solution.py:558
  109.8 34.7 %copy-start.4 = (f32[264,128]{1,0:T(8,128)}, f32[264,128]{1,0:T(8,128)S(1)}, u32[]{:S(2)}) copy-start(f32[264,128]{1,0:T(8,128)S(1)} %collective-permute-done.4.refs_3_) | copy-start | bytes 405508
  109.8 8.8 %collective-permute-start.9 = (f32[264,128]{1,0:T(8,128)}, f32[264,128]{1,0:T(8,128)S(1)}, u32[]{:S(2)}, u32[]{:S(2)}) collective-permute-start(f32[264,128]{1,0:T(8,128)} %get-tuple-element.38), channel_id=1, source_target_pairs={{0,16},{1,17},{2,18},{3,19},{8,24},{9,25},{10,26},{11,27},{16,0},{... | collective-permute-start | bytes 405512 | tf_op jit(solution)/shard_map/ppermute | solution.py:558
  111.3 33.3 %copy-start.5 = (f32[264,128]{1,0:T(8,128)}, f32[264,128]{1,0:T(8,128)S(1)}, u32[]{:S(2)}) copy-start(f32[264,128]{1,0:T(8,128)S(1)} %collective-permute-done.5.refs_4_) | copy-start | bytes 405508
  111.3 13.7 %collective-permute-start.10 = (f32[264,128]{1,0:T(8,128)}, f32[264,128]{1,0:T(8,128)S(1)}, u32[]{:S(2)}, u32[]{:S(2)}) collective-permute-start(f32[264,128]{1,0:T(8,128)} %get-tuple-element.39), channel_id=1, source_target_pairs={{0,17},{1,16},{2,19},{3,18},{8,25},{9,24},{10,27},{11,26},{16,1},{... | collective-permute-start | bytes 405512 | tf_op jit(solution)/shard_map/ppermute | solution.py:558
  112.8 31.8 %copy-start.6 = (f32[264,128]{1,0:T(8,128)}, f32[264,128]{1,0:T(8,128)S(1)}, u32[]{:S(2)}) copy-start(f32[264,128]{1,0:T(8,128)S(1)} %collective-permute-done.6.refs_5_) | copy-start | bytes 405508
  112.8 13.0 %collective-permute-start.11 = (f32[264,128]{1,0:T(8,128)}, f32[264,128]{1,0:T(8,128)S(1)}, u32[]{:S(2)}, u32[]{:S(2)}) collective-permute-start(f32[264,128]{1,0:T(8,128)} %get-tuple-element.40), channel_id=1, source_target_pairs={{0,18},{1,19},{2,16},{3,17},{8,26},{9,27},{10,24},{11,25},{16,2},{... | collective-permute-start | bytes 405512 | tf_op jit(solution)/shard_map/ppermute | solution.py:558
  114.1 30.5 %copy-start.7 = (f32[264,128]{1,0:T(8,128)}, f32[264,128]{1,0:T(8,128)S(1)}, u32[]{:S(2)}) copy-start(f32[264,128]{1,0:T(8,128)S(1)} %collective-permute-done.7.refs_6_) | copy-start | bytes 405508
  114.1 17.4 %collective-permute-start.12 = (f32[264,128]{1,0:T(8,128)}, f32[264,128]{1,0:T(8,128)}, u32[]{:S(2)}, u32[]{:S(2)}) collective-permute-start(f32[264,128]{1,0:T(8,128)} %get-tuple-element.41), channel_id=1, source_target_pairs={{0,19},{1,18},{2,17},{3,16},{8,27},{9,26},{10,25},{11,24},{16,3},{... | collective-permute-start | bytes 405512 | tf_op jit(solution)/shard_map/ppermute | solution.py:558
  117.4 27.1 %copy-start.8 = (f32[264,128]{1,0:T(8,128)}, f32[264,128]{1,0:T(8,128)S(1)}, u32[]{:S(2)}) copy-start(f32[264,128]{1,0:T(8,128)S(1)} %collective-permute-done.8.refs_7_) | copy-start | bytes 405508
  117.4 14.0 %collective-permute-start.13 = (f32[264,128]{1,0:T(8,128)}, f32[264,128]{1,0:T(8,128)}, u32[]{:S(2)}, u32[]{:S(2)}) collective-permute-start(f32[264,128]{1,0:T(8,128)} %get-tuple-element.42), channel_id=1, source_target_pairs={{0,24},{1,25},{2,26},{3,27},{8,16},{9,17},{10,18},{11,19},{16,8},{... | collective-permute-start | bytes 405512 | tf_op jit(solution)/shard_map/ppermute | solution.py:558
  118.6 26.0 %copy-start.9 = (f32[264,128]{1,0:T(8,128)}, f32[264,128]{1,0:T(8,128)S(1)}, u32[]{:S(2)}) copy-start(f32[264,128]{1,0:T(8,128)S(1)} %collective-permute-done.9.refs_8_) | copy-start | bytes 405508
  118.6 16.7 %collective-permute-start.14 = (f32[264,128]{1,0:T(8,128)}, f32[264,128]{1,0:T(8,128)}, u32[]{:S(2)}, u32[]{:S(2)}) collective-permute-start(f32[264,128]{1,0:T(8,128)} %get-tuple-element.43), channel_id=1, source_target_pairs={{0,25},{1,24},{2,27},{3,26},{8,17},{9,16},{10,19},{11,18},{16,9},{... | collective-permute-start | bytes 405512 | tf_op jit(solution)/shard_map/ppermute | solution.py:558
  125.0 19.6 %copy-start.10 = (f32[264,128]{1,0:T(8,128)}, f32[264,128]{1,0:T(8,128)S(1)}, u32[]{:S(2)}) copy-start(f32[264,128]{1,0:T(8,128)S(1)} %collective-permute-done.10.refs_9_) | copy-start | bytes 405508
  125.0 10.2 %collective-permute-start.15 = (f32[264,128]{1,0:T(8,128)}, f32[264,128]{1,0:T(8,128)}, u32[]{:S(2)}, u32[]{:S(2)}) collective-permute-start(f32[264,128]{1,0:T(8,128)} %get-tuple-element.44), channel_id=1, source_target_pairs={{0,26},{1,27},{2,24},{3,25},{8,18},{9,19},{10,16},{11,17},{16,10},... | collective-permute-start | bytes 405512 | tf_op jit(solution)/shard_map/ppermute | solution.py:558
  125.8 18.8 %copy-start.11 = (f32[264,128]{1,0:T(8,128)}, f32[264,128]{1,0:T(8,128)S(1)}, u32[]{:S(2)}) copy-start(f32[264,128]{1,0:T(8,128)S(1)} %collective-permute-done.11.refs_10_) | copy-start | bytes 405508
  125.8 9.5 %collective-permute-start.16 = (f32[264,128]{1,0:T(8,128)}, f32[264,128]{1,0:T(8,128)}, u32[]{:S(2)}, u32[]{:S(2)}) collective-permute-start(f32[264,128]{1,0:T(8,128)} %get-tuple-element.45), channel_id=1, source_target_pairs={{0,27},{1,26},{2,25},{3,24},{8,19},{9,18},{10,17},{11,16},{16,11},... | collective-permute-start | bytes 405512 | tf_op jit(solution)/shard_map/ppermute | solution.py:558
  150.7 1.3 copy-start
